TPU v7x, 32 devices: a whole 2x2x4 slice. The times are simulated.
32 devices in a mesh: blk: 8 (over y, x, core), ulysses: 4 (over z).
Axes of the slice: x: 2, y: 2, z: 4, core: 2. Of those that a mesh axis runs over, the one named last changes fastest.
Arguments:
- tokens: bfloat16 [2048, 3072], P(('blk', 'ulysses')), may hold values from -6 to 6
- mod_shift: float32 [3072], replicated, may hold values from -3 to 3
- mod_scale: float32 [3072], replicated, may hold values from -3 to 3
- mod_gate: float32 [3072], replicated, may hold values from 0.5 to 1.5
- qkv_weight: bfloat16 [3, 3072, 3072], P(None, None, 'ulysses'), may hold values from -0.109375 to 0.109375
- query_gain: float32 [128], replicated, may hold values from 1 to 16
- key_gain: float32 [128], replicated, may hold values from 1 to 16
- out_weight: bfloat16 [3072, 3072], P(None, 'ulysses'), may hold values from -0.109375 to 0.109375
Outputs:
- mixed: bfloat16 [2048, 3072], P(('blk', 'ulysses'))
All inputs are finite; a program needn't handle non-finite values.
Results may differ from a plain program's by a relative error of at most 0.013.
The roundings to bfloat16 on the way count: a program that leaves them out, or rounds other values in their place, can miss the bound.
Values may be sent and summed in bfloat16 or wider, within the bound.
No kernel may reach another device: no remote copies, remote signals or barrier semaphores. Data moves between devices by JAX's collectives and lax.ppermute only.
A program may use at most 128 MiB of HBM per device.

v0:
```python
import math
import jax
import jax.numpy as jnp
from jax import lax
from jax.sharding import PartitionSpec as P


def head_norm(projected, gain, factor):
    split = projected.reshape(projected.shape[0], -1, gain.shape[0])
    meansq = jnp.mean(split * split, axis=-1, keepdims=True)
    return (split * lax.rsqrt(meansq + 1e-06) * gain * factor).reshape(projected.shape)


def local(tokens, mod_shift, mod_scale, mod_gate, qkv_weight, query_gain, key_gain, out_weight):
    wide = tokens.astype(jnp.float32)
    center = jnp.mean(wide, axis=-1, keepdims=True)
    spread = jnp.mean((wide - center) ** 2, axis=-1, keepdims=True)
    normed = (wide - center) / jnp.sqrt(spread + 1e-06)
    modulated = (normed * (1.0 + mod_scale) + mod_shift).astype(jnp.bfloat16)
    head_size = query_gain.shape[0]
    local_width = qkv_weight.shape[2]
    heads_here = local_width // head_size
    factor = 1.0 / math.sqrt(head_size)
    sums = jnp.einsum(
        "rd,jde->jre",
        lax.all_gather(modulated, "ulysses", axis=0, tiled=True),
        qkv_weight,
        preferred_element_type=jnp.float32,
    )
    queries = head_norm(sums[0], query_gain, factor)
    keys = head_norm(sums[1], key_gain, 1.0)
    stacked = jnp.stack([queries, keys, sums[2]]).astype(jnp.bfloat16)
    queries, keys, values = (stacked[0], stacked[1], stacked[2])
    query_rows = queries.shape[0]
    query_heads = queries.reshape(query_rows, heads_here, head_size)
    start_state = (
        jnp.full((heads_here, query_rows), -1e30, jnp.float32),
        jnp.zeros((heads_here, query_rows), jnp.float32),
        jnp.zeros((heads_here, query_rows, head_size), jnp.float32),
    )
    key_part = lax.all_gather(keys, "blk", axis=0, tiled=True)
    value_part = lax.all_gather(values, "blk", axis=0, tiled=True)
    count = key_part.shape[0] // query_rows

    def step(position, state):
        highest, total, numerator = state
        key_block = lax.dynamic_slice_in_dim(key_part, position * query_rows, query_rows, 0)
        value_block = lax.dynamic_slice_in_dim(value_part, position * query_rows, query_rows, 0)
        key_block = key_block.reshape(query_rows, heads_here, head_size)
        value_block = value_block.reshape(query_rows, heads_here, head_size)
        scores = jnp.einsum(
            "qhd,khd->hqk", query_heads, key_block, preferred_element_type=jnp.float32
        )
        new_high = jnp.maximum(highest, jnp.max(scores, axis=-1))
        rescale = jnp.exp(highest - new_high)
        powers = jnp.exp(scores - new_high[..., None])
        total = total * rescale + jnp.sum(powers, axis=-1)
        numerator = numerator * rescale[..., None] + jnp.einsum(
            "hqk,khd->hqd",
            powers.astype(jnp.bfloat16),
            value_block,
            preferred_element_type=jnp.float32,
        )
        return (new_high, total, numerator)

    highest, total, numerator = lax.fori_loop(0, count, step, start_state)
    attended = (numerator / total[..., None]).transpose(1, 0, 2).reshape(query_rows, local_width)
    attended = attended.astype(jnp.bfloat16)
    columns = jnp.dot(
        lax.all_gather(attended, "ulysses", axis=1, tiled=True),
        out_weight,
        preferred_element_type=jnp.float32,
    )
    branch = lax.all_to_all(
        columns.astype(jnp.bfloat16), "ulysses", split_axis=0, concat_axis=1, tiled=True
    ).astype(columns.dtype)
    return (wide + mod_gate * branch).astype(jnp.bfloat16)


def solution(mesh):
    in_specs = (
        P(("blk", "ulysses"), None),
        P(),
        P(),
        P(),
        P(None, None, "ulysses"),
        P(),
        P(),
        P(None, "ulysses"),
    )
    out_specs = P(("blk", "ulysses"), None)
    return jax.shard_map(local, mesh=mesh, in_specs=in_specs, out_specs=out_specs, check_vma=False)
```

profile of v0, /device:TPU:0, one launch (start us, length us, event | category | flops | bytes accessed | tf_op | source)
XLA Modules:
  0.0 214.0 jit_solution(12685129563109106059)
XLA Ops:
  6.5 1.1 convert_reduce_fusion
  7.7 1.3 fusion.9
  9.0 0.7 broadcast_add_fusion
  9.7 2.0 fusion.12
  11.8 39.8 %all-gather.7.cloned.1.call-done = bf16[256,3072]{1,0:T(8,128)(2,1)} async-done(((bf16[64,3072]{1,0:T(8,128)(2,1)}), bf16[256,3072]{1,0:T(8,128)(2,1)}) %all-gather.7.cloned.1.call-update) | async-done | bytes 1572880 | tf_op jit(solution)/shard_map/all_gather | solution.py:26
  51.6 7.9 %convolution_bitcast_fusion = f32[3,256,768]{2,1,0:T(8,128)S(1)} fusion(bf16[3,3072,768]{2,1,0:T(8,128)(2,1)} %param.14, bf16[256,3072]{1,0:T(8,128)(2,1)} %all-gather.7.cloned.1.call-done), kind=kOutput, calls=%fused_computation.14 | convolution fusion | flops 3623878656 | bytes 18087936 | tf_op jit(solution)/shard_map/rd,jde->jre/dot_general | solution.py:24
  59.5 0.8 slice.32
  60.3 1.2 slice_multiply_fusion
  61.6 1.4 copy.30
  63.1 1.2 copy.31
  64.3 1.4 copy.28
  65.9 1.1 copy.29
  67.0 2.4 %multiply_convert_fusion = (bf16[1,256,768]{2,1,0:T(8,128)(2,1)S(1)}, bf16[1,256,768]{2,1,0:T(8,128)(2,1)}) fusion(f32[1,256,768]{2,1,0:T(8,128)} %copy.31, f32[3,256,768]{2,1,0:T(8,128)S(1)} %convolution_bitcast_fusion, f32[768]{0:T(1024)S(1)} %get-tuple-element.201, f32[768]{0:T(1024)S(1)} %get-tuple-element.202, f32[1,256,768]{2,1,0:T(8,128)} %copy.29), kind=kLoop, calls=%fused_computation.30 | loop fusion | flops 1376256 | bytes 3938304 | tf_op jit(solution)/shard_map/slice | solution.py:33
  69.9 21.6 %all-gather.13.cloned.1.call-done = bf16[1,2048,768]{2,1,0:T(8,128)(2,1)} async-done(((bf16[1,256,768]{2,1,0:T(8,128)(2,1)}), bf16[1,2048,768]{2,1,0:T(8,128)(2,1)}) %all-gather.13.cloned.1.call-update) | async-done | bytes 3145744 | tf_op jit(solution)/shard_map/all_gather | solution.py:42
  91.5 34.1 %all-gather.11.cloned.1.call-done = bf16[1,2048,768]{2,1,0:T(8,128)(2,1)} async-done(((bf16[1,256,768]{2,1,0:T(8,128)(2,1)}), bf16[1,2048,768]{2,1,0:T(8,128)(2,1)}) %all-gather.11.cloned.1.call-update) | async-done | bytes 3145744 | tf_op jit(solution)/shard_map/all_gather | solution.py:41
  125.6 23.6 %while.18 = (s32[]{:T(128)}, f32[6,256]{1,0:T(8,128)S(1)}, f32[6,256]{1,0:T(8,128)S(1)}, f32[6,256,128]{2,1,0:T(8,128)S(1)}, bf16[2048,768]{1,0:T(8,128)(2,1)}, ...) while((s32[]{:T(128)}, f32[6,256]{1,0:T(8,128)S(1)}, ...), condition=%wide.region_7.0_spmd.clone, body=%wide.region_4.0_spmd.clone.sunk | while | flops 203890176 | bytes 10715315 | solution.py:66
  125.6 1.2 constant_dynamic-slice_fusion.3
  128.5 1.2 constant_dynamic-slice_fusion.3
  130.7 0.7 convolution_add_fusion.2
  131.5 1.2 constant_dynamic-slice_fusion.3
  133.7 0.7 convolution_add_fusion.2
  134.4 1.2 constant_dynamic-slice_fusion.3
  137.4 1.2 constant_dynamic-slice_fusion.3
  140.3 1.2 constant_dynamic-slice_fusion.3
  143.3 1.2 constant_dynamic-slice_fusion.3
  146.2 1.2 constant_dynamic-slice_fusion.3
  149.4 0.8 divide_convert_fusion
  150.2 37.2 %all-gather.9.cloned.1.call-done = bf16[256,3072]{0,1:T(8,128)(2,1)} async-done(((bf16[256,768]{0,1:T(8,128)(2,1)}), bf16[256,3072]{0,1:T(8,128)(2,1)}) %all-gather.9.cloned.1.call-update) | async-done | bytes 1572880 | tf_op jit(solution)/shard_map/all_gather | solution.py:70
  187.4 4.2 %convolution_convert_fusion = bf16[256,768]{1,0:T(8,128)(2,1)S(1)} fusion(bf16[256,3072]{0,1:T(8,128)(2,1)} %all-gather.9.cloned.1.call-done, bf16[3072,768]{1,0:T(8,128)(2,1)} %param.17), kind=kOutput, calls=%fused_computation.16 | convolution fusion | flops 1208156160 | bytes 6684672 | tf_op jit(solution)/shard_map/dot_general | solution.py:69
  191.7 13.9 %all_to_all.13 = bf16[4,64,768]{2,1,0:T(8,128)(2,1)S(1)} all-to-all(bf16[4,64,768]{2,1,0:T(8,128)(2,1)S(1)} %bitcast.69), channel_id=1, replica_groups=mesh['blk'=8,'ulysses'=4] {'ulysses'}, dimensions={0} | all-to-all | bytes 786432 | tf_op jit(solution)/shard_map/all_to_all | solution.py:74
  205.7 0.9 copy-done
  206.6 0.8 fusion.13
  (94 shorter events, 13.5 us)
Async XLA Ops:
  6.5 45.1 %all-gather.7.cloned.1.call-start = ((), (), s32[]{:S(2)}) async-start(), calls=%async_computation.1 | async-start | bytes 1966080 | tf_op jit(solution)/shard_map/all_gather | solution.py:26
  11.7 48.6 %copy-start.2 = (f32[128]{0:T(128)S(1)}, f32[128]{0:T(128)}, u32[]{:S(2)}) copy-start(f32[128]{0:T(128)} %param.15) | copy-start | bytes 1540
  11.7 48.6 %copy-start.3 = (f32[128]{0:T(128)S(1)}, f32[128]{0:T(128)}, u32[]{:S(2)}) copy-start(f32[128]{0:T(128)} %param.16) | copy-start | bytes 1540
  11.7 79.8 %all-gather.13.cloned.1.call-start = ((), (), s32[]{:S(2)}) async-start(), calls=%async_computation.4 | async-start | bytes 3538944 | tf_op jit(solution)/shard_map/all_gather | solution.py:42
  60.3 65.3 %all-gather.11.cloned.1.call-start = ((), (), s32[]{:S(2)}) async-start(), calls=%async_computation.3 | async-start | bytes 3538944 | tf_op jit(solution)/shard_map/all_gather | solution.py:41
  69.4 118.0 %all-gather.9.cloned.1.call-start = ((), (), s32[]{:S(2)}) async-start(), calls=%async_computation.2 | async-start | bytes 1966080 | tf_op jit(solution)/shard_map/all_gather | solution.py:70
  205.6 1.0 copy-start
  205.6 1.0 copy-start.1
Sparse Core Ops, SparseCore 0:
  11.8 39.7 all-gather.6
  60.4 31.0 all-gather.12
  93.4 32.1 all-gather.10
  150.4 37.0 all-gather.8
where the time goes:
time: 215 us; the launch traced here: 214 us
  waiting for transfers between devices  133 us (62%)
  matrix products  21 us (10%)
  local copies, waits for them, and re-layouts  19.7 us (9%)
  blocking collectives  13.9 us (6%)
  between operations  13.3 us (6%)
  other arithmetic  12.5 us (6%)
    all_gather x1, waiting for transfers between devices, local(): lax.all_gather(modulated, 'ulysses', axis=0, tiled=True)  39.8 us
    all_gather x1, waiting for transfers between devices, local(): lax.all_gather(attended, 'ulysses', axis=1, tiled=True)  37.2 us
    all_gather x1, waiting for transfers between devices, local(): key_part = lax.all_gather(keys, 'blk', axis=0, tiled=True)  34.1 us
    all_gather x1, waiting for transfers between devices, local(): value_part = lax.all_gather(values, 'blk', axis=0, tiled=True)  21.6 us
    all_to_all x1, blocking collectives, local(): lax.all_to_all(columns.astype(jnp.bfloat16), 'ulysses', split_axis=0, con...  13.9 us
    dynamic_slice x16, local copies, waits for them, and re-layouts, step(): lax.dynamic_slice_in_dim(value_part, position * query_rows, query_rows, 0)  10.7 us
    dot_general x1, matrix products, local(): jnp.einsum('rd,jde->jre', lax.all_gather(modulated, 'ulysses', axis=0, ti...  7.86 us
    dot_general x8, matrix products, step(): jnp.einsum('hqk,khd->hqd', powers.astype(jnp.bfloat16), value_block, pref...  5.52 us
  transfers between devices with their start and end apart: 4, of which 4 were waited for; matrix products, arithmetic and copies ran while one was open for 4% of the time, Pallas kernels for 0%

commit v1 on v0

--- a/solution.py
+++ b/solution.py
@@ -38,8 +38,11 @@
         jnp.zeros((heads_here, query_rows), jnp.float32),
         jnp.zeros((heads_here, query_rows, head_size), jnp.float32),
     )
-    key_part = lax.all_gather(keys, "blk", axis=0, tiled=True)
-    value_part = lax.all_gather(values, "blk", axis=0, tiled=True)
+    key_part, value_part = jnp.split(
+        lax.all_gather(jnp.concatenate([keys, values], axis=1), "blk", axis=0, tiled=True),
+        [keys.shape[1]],
+        axis=1,
+    )
     count = key_part.shape[0] // query_rows
 
     def step(position, state):

time: 215 us -> 223 us (1.037)
  local copies, waits for them, and re-layouts: 19.7 us -> 33.5 us
  waiting for transfers between devices: 133 us -> 121 us
  other arithmetic: 12.5 us -> 17.5 us
    all_gather x2 -> x1, waiting for transfers between devices: 55.7 us -> 43.9 us  [local(): lax.all_gather(jnp.concatenate([keys, values], axis=1), 'blk', axis=0, ti...]
    while x8 -> x56, local copies, waits for them, and re-layouts: 0.02 us -> 8.29 us
    split x0 -> x1, local copies, waits for them, and re-layouts: none -> 5.88 us  [local(): jnp.split(lax.all_gather(jnp.concatenate([keys, values], axis=1), 'blk',...]
    add x8, other arithmetic: 0.1 us -> 4.95 us  [step(): total = total * rescale + jnp.sum(powers, axis=-1)]
  transfers between devices with their start and end apart: 4 -> 3, of which waited for: 4 -> 3; matrix products, arithmetic and copies ran while one was open for 4% -> 0% of each run, Pallas kernels for 0% -> 0%
where the time goes in v1:
time: 223 us; the launch traced here: 221 us
  waiting for transfers between devices  121 us (54%)
  local copies, waits for them, and re-layouts  33.5 us (15%)
  matrix products  21 us (9%)
  other arithmetic  17.5 us (8%)
  blocking collectives  13.9 us (6%)
  between operations  13.3 us (6%)
    all_gather x1, waiting for transfers between devices, local(): lax.all_gather(jnp.concatenate([keys, values], axis=1), 'blk', axis=0, ti...  43.9 us
    all_gather x1, waiting for transfers between devices, local(): lax.all_gather(modulated, 'ulysses', axis=0, tiled=True)  39.8 us
    all_gather x1, waiting for transfers between devices, local(): lax.all_gather(attended, 'ulysses', axis=1, tiled=True)  37.2 us
    all_to_all x1, blocking collectives, local(): lax.all_to_all(columns.astype(jnp.bfloat16), 'ulysses', split_axis=0, con...  13.9 us
    dynamic_slice x16, local copies, waits for them, and re-layouts, step(): lax.dynamic_slice_in_dim(value_part, position * query_rows, query_rows, 0)  10.7 us
    while x56, local copies, waits for them, and re-layouts  8.29 us
    dot_general x1, matrix products, local(): jnp.einsum('rd,jde->jre', lax.all_gather(modulated, 'ulysses', axis=0, ti...  7.86 us
    split x1, local copies, waits for them, and re-layouts, local(): jnp.split(lax.all_gather(jnp.concatenate([keys, values], axis=1), 'blk',...  5.88 us
  transfers between devices with their start and end apart: 3, of which 3 were waited for; matrix products, arithmetic and copies ran while one was open for 0% of the time, Pallas kernels for 0%

profile of v1, /device:TPU:0, one launch (start us, length us, event | category | flops | bytes accessed | tf_op | source)
XLA Modules:
  0.0 221.2 jit_solution(2813152202219448426)
XLA Ops:
  6.5 1.2 convert_reduce_fusion
  7.7 1.3 fusion.9
  9.0 0.7 broadcast_add_fusion
  9.7 2.0 fusion.12
  11.8 39.8 %all-gather.4.cloned.1.call-done = bf16[256,3072]{1,0:T(8,128)(2,1)} async-done(((bf16[64,3072]{1,0:T(8,128)(2,1)}), bf16[256,3072]{1,0:T(8,128)(2,1)}) %all-gather.4.cloned.1.call-update) | async-done | bytes 1572880 | tf_op jit(solution)/shard_map/all_gather | solution.py:26
  51.6 7.9 %convolution_bitcast_fusion = f32[3,256,768]{2,1,0:T(8,128)S(1)} fusion(bf16[3,3072,768]{2,1,0:T(8,128)(2,1)} %param.14, bf16[256,3072]{1,0:T(8,128)(2,1)} %all-gather.4.cloned.1.call-done), kind=kOutput, calls=%fused_computation.14 | convolution fusion | flops 3623878656 | bytes 18087936 | tf_op jit(solution)/shard_map/rd,jde->jre/dot_general | solution.py:24
  59.5 1.3 slice_multiply_fusion
  60.8 1.4 copy.28
  62.3 1.2 copy.29
  63.5 1.4 copy.30
  65.1 1.2 copy.31
  66.2 1.6 multiply_convert_fusion
  67.8 0.9 pad_maximum_fusion
  69.2 43.9 %all-gather.6.cloned.1.call-done = bf16[2048,1536]{1,0:T(8,128)(2,1)} async-done(((bf16[256,1536]{1,0:T(8,128)(2,1)}), bf16[2048,1536]{1,0:T(8,128)(2,1)}) %all-gather.6.cloned.1.call-update) | async-done | bytes 6291472 | tf_op jit(solution)/shard_map/all_gather | solution.py:42
  113.2 5.9 %fusion.16 = (bf16[2048,768]{1,0:T(8,128)(2,1)}, bf16[2048,768]{1,0:T(8,128)(2,1)}) fusion(bf16[2048,1536]{1,0:T(8,128)(2,1)} %all-gather.6.cloned.1.call-done), kind=kLoop, calls=%fused_computation.44 | loop fusion | bytes 12582912 | tf_op jit(solution)/shard_map/split | solution.py:41
  119.0 36.9 %while.18 = (s32[]{:T(128)}, f32[6,256]{1,0:T(8,128)S(1)}, f32[6,256]{1,0:T(8,128)}, f32[6,256,128]{2,1,0:T(8,128)S(1)}, bf16[2048,768]{1,0:T(8,128)(2,1)}, /*in...) while((s32[]{:T(128)}, f32[6,256]{1,0:T(8,128)S(1)}, ...), condition=%wide.region_7.0_spmd.clone, body=%wide.region_4.0_spmd.clone.sunk | while | flops 203890176 | bytes 10789119 | solution.py:69
  119.0 1.2 constant_dynamic-slice_fusion.3
  123.1 1.2 constant_dynamic-slice_fusion.3
  127.8 1.2 constant_dynamic-slice_fusion.3
  130.2 0.7 fusion.34
  132.5 1.2 constant_dynamic-slice_fusion.3
  134.9 0.7 fusion.34
  137.2 1.2 constant_dynamic-slice_fusion.3
  141.9 1.2 constant_dynamic-slice_fusion.3
  146.6 1.2 constant_dynamic-slice_fusion.3
  151.3 1.2 constant_dynamic-slice_fusion.3
  156.6 0.8 divide_convert_fusion
  157.5 37.2 %all-gather.8.cloned.1.call-done = bf16[256,3072]{0,1:T(8,128)(2,1)} async-done(((bf16[256,768]{0,1:T(8,128)(2,1)}), bf16[256,3072]{0,1:T(8,128)(2,1)}) %all-gather.8.cloned.1.call-update) | async-done | bytes 1572880 | tf_op jit(solution)/shard_map/all_gather | solution.py:73
  194.7 4.2 %convolution_convert_fusion = bf16[256,768]{1,0:T(8,128)(2,1)S(1)} fusion(bf16[256,3072]{0,1:T(8,128)(2,1)} %all-gather.8.cloned.1.call-done, bf16[3072,768]{1,0:T(8,128)(2,1)} %param.17), kind=kOutput, calls=%fused_computation.16 | convolution fusion | flops 1208156160 | bytes 6684672 | tf_op jit(solution)/shard_map/dot_general | solution.py:72
  198.9 13.9 %all_to_all.13 = bf16[4,64,768]{2,1,0:T(8,128)(2,1)S(1)} all-to-all(bf16[4,64,768]{2,1,0:T(8,128)(2,1)S(1)} %bitcast.69), channel_id=1, replica_groups=mesh['blk'=8,'ulysses'=4] {'ulysses'}, dimensions={0} | all-to-all | bytes 786432 | tf_op jit(solution)/shard_map/all_to_all | solution.py:77
  213.0 0.9 copy-done
  213.8 0.8 fusion.13
  (143 shorter events, 26.9 us)
Async XLA Ops:
  6.5 5.2 %copy-start.6 = (f32[128]{0:T(128)S(1)}, f32[128]{0:T(128)}, u32[]{:S(2)}) copy-start(f32[128]{0:T(128)} %param.15) | copy-start | bytes 1540
  6.5 5.2 %copy-start.7 = (f32[128]{0:T(128)S(1)}, f32[128]{0:T(128)}, u32[]{:S(2)}) copy-start(f32[128]{0:T(128)} %param.16) | copy-start | bytes 1540
  6.5 45.1 %all-gather.4.cloned.1.call-start = ((), (), s32[]{:S(2)}) async-start(), calls=%async_computation.1 | async-start | bytes 1966080 | tf_op jit(solution)/shard_map/all_gather | solution.py:26
  11.7 101.4 %all-gather.6.cloned.1.call-start = ((), (), s32[]{:S(2)}) async-start(), calls=%async_computation.2 | async-start | bytes 7077888 | tf_op jit(solution)/shard_map/all_gather | solution.py:42
  68.8 125.9 %all-gather.8.cloned.1.call-start = ((), (), s32[]{:S(2)}) async-start(), calls=%async_computation.3 | async-start | bytes 1966080 | tf_op jit(solution)/shard_map/all_gather | solution.py:73
  119.0 1.8 copy-start.1
  120.8 0.7 copy-start.2
  121.5 0.6 copy-start.3
  123.0 1.8 copy-start.1
  124.8 0.7 copy-start.2
  126.2 0.6 copy-start.3
  127.7 1.8 copy-start.1
  129.5 0.7 copy-start.2
  130.9 0.6 copy-start.3
  132.4 1.8 copy-start.1
  134.2 0.7 copy-start.2
  135.6 0.6 copy-start.3
  137.1 1.8 copy-start.1
  138.9 0.7 copy-start.2
  140.4 0.6 copy-start.3
  141.8 1.8 copy-start.1
  143.6 0.7 copy-start.2
  145.1 0.6 copy-start.3
  146.5 1.8 copy-start.1
  148.3 0.7 copy-start.2
  149.8 0.6 copy-start.3
  151.2 1.8 copy-start.1
  153.0 0.7 copy-start.2
  154.5 0.6 copy-start.3
  155.9 0.7 copy-start.4
  212.8 1.0 copy-start
  212.8 1.0 copy-start.5
Sparse Core Ops, SparseCore 0:
  11.8 39.7 all-gather.3
  68.9 44.2 all-gather.5
  157.6 37.0 all-gather.7
